TPU v7x, 32 devices: a whole 2x2x4 slice. The times are simulated.
32 devices in a mesh: node: 8 (over y, x, core), local: 4 (over z).
Axes of the slice: x: 2, y: 2, z: 4, core: 2. Of those that a mesh axis runs over, the one named last changes fastest.
Arguments:
- tokens: bfloat16 [32, 7168], P(('node', 'local')), may hold values from -6 to 6
- w_gate: bfloat16 [16, 1024, 7168], P('node', 'local'), may hold values from -0.0625 to 0.0625
- w_up: bfloat16 [16, 1024, 7168], P('node', 'local'), may hold values from -0.0625 to 0.0625
- w_down: bfloat16 [16, 1024, 7168], P('node', 'local'), may hold values from -0.1875 to 0.1875
- expert_ids: int32 [32, 8], P(('node', 'local')), may hold values from 0 to 15, all different within a row
- gate_ints: int32 [32, 8], P(('node', 'local')), may hold values from 1 to 8
Outputs:
- mixed: bfloat16 [32, 7168], P(('node', 'local'))
Inputs may be any that keep to these rules, and one draw needn't show every extreme that they name: `expert_ids`: each row names 8 different experts.
All inputs are finite; a program needn't handle non-finite values.
Results may differ from a plain program's by a relative error of at most 0.025.
Values may be sent and summed in bfloat16 or wider, within the bound.
A program may use at most 64 MiB of HBM per device.

v0:
```python
import jax
import jax.numpy as jnp
from jax import lax
from jax.sharding import PartitionSpec as P

CAP = 8


def on_device(tokens, w_gate, w_up, w_down, expert_ids, gate_ints):
    node_count = lax.axis_size("node")
    tok_dev = tokens.shape[0]
    model_width = tokens.shape[1]
    exp_node = w_gate.shape[0]
    slot_count = node_count * tok_dev
    wanted = jnp.arange(node_count * exp_node, dtype=jnp.int32).reshape(node_count, exp_node)
    matched = expert_ids[None, :, :, None] == wanted[:, None, None, :]
    gate_sums = jnp.sum(jnp.where(matched, gate_ints[None, :, :, None], 0), axis=2)
    is_hit = jnp.sum(gate_sums, axis=-1) > 0
    outgoing = jnp.where(is_hit[:, :, None], tokens[None, :, :], jnp.zeros_like(tokens)[None, :, :])
    rows_in, gates_in = (
        lax.all_to_all(outgoing, "node", split_axis=0, concat_axis=0, tiled=True),
        lax.all_to_all(
            gate_sums.astype(jnp.bfloat16), "node", split_axis=0, concat_axis=0, tiled=True
        ),
    )
    flat_rows = rows_in.reshape(slot_count, model_width)
    flat_gates = gates_in.reshape(slot_count, exp_node)
    present = (jnp.sum(flat_gates.astype(jnp.float32), axis=-1) > 0).astype(jnp.int32)
    slot_rank = jnp.cumsum(present) - present
    picker = (
        (present[None, :] > 0) & (slot_rank[None, :] == jnp.arange(CAP, dtype=jnp.int32)[:, None])
    ).astype(jnp.bfloat16)
    packed = jnp.dot(picker, flat_rows, preferred_element_type=jnp.float32).astype(jnp.bfloat16)
    packed_gates = jnp.dot(picker, flat_gates, preferred_element_type=jnp.float32).astype(
        jnp.bfloat16
    )
    all_rows, all_gates = (
        lax.all_gather(packed, "local", axis=0, tiled=True),
        lax.all_gather(packed_gates, "local", axis=0, tiled=True),
    )
    gate_act = jnp.einsum("rd,efd->ref", all_rows, w_gate, preferred_element_type=jnp.float32)
    up_act = jnp.einsum("rd,efd->ref", all_rows, w_up, preferred_element_type=jnp.float32)
    scales = all_gates.astype(jnp.float32) / 8.0
    hidden = (jax.nn.silu(gate_act) * up_act * scales[:, :, None]).astype(jnp.bfloat16)
    hidden = hidden.reshape(hidden.shape[0], -1)
    down_flat = w_down.reshape(-1, model_width)
    partial_value = jnp.dot(hidden, down_flat, preferred_element_type=jnp.float32)
    summed = lax.psum_scatter(
        partial_value.astype(jnp.bfloat16), "local", scatter_dimension=0, tiled=True
    )
    unpacked = jnp.dot(picker.T, summed, preferred_element_type=jnp.float32).astype(jnp.bfloat16)
    unpacked = unpacked.reshape(node_count, tok_dev, model_width)
    returned = lax.all_to_all(unpacked, "node", split_axis=0, concat_axis=0, tiled=True)
    return jnp.sum(returned.astype(jnp.float32), axis=0).astype(jnp.bfloat16)


def solution(mesh):
    return jax.shard_map(
        on_device,
        mesh=mesh,
        in_specs=(
            P(("node", "local"), None),
            P("node", "local", None),
            P("node", "local", None),
            P("node", "local", None),
            P(("node", "local"), None),
            P(("node", "local"), None),
        ),
        out_specs=P(("node", "local"), None),
        check_vma=False,
    )
```

profile of v0, /device:TPU:0, one launch (start us, length us, event | category | flops | bytes accessed | tf_op | source)
XLA Modules:
  0.0 101.5 jit_solution(9344661517451039057)
XLA Ops:
  6.5 1.0 select_reduce_fusion.1
  7.5 0.7 copy.17
  8.2 5.2 %all-to-all-start = ((bf16[8,1,2]{2,1,0:T(2,128)(2,1)}), bf16[8,1,2]{2,1,0:T(2,128)(2,1)S(1)}, u32[]{:S(2)}, u32[]{:S(2)}) async-start(bf16[8,1,2]{2,1,0:T(2,128)(2,1)} %copy.17), calls=%async_computation | async-start | bytes 8192 | tf_op jit(solution)/shard_map/all_to_all | solution.py:22
  13.4 0.8 reduce.5
  14.3 0.2 broadcast_select_fusion
  14.5 0.5 broadcast.174
  15.0 1.2 %reduce.6 = bf16[8,7168]{1,0:T(8,128)(2,1)S(1)} reduce(bf16[8,1,7168]{2,1,0:T(2,128)(2,1)S(1)} %broadcast_select_fusion, bf16[]{:T(256)} %broadcast.174), dimensions={1}, to_apply=%broadcast_select_fusion.reduce_sub_computation | reduce | bytes 229378 | tf_op jit(solution)/shard_map/jit(_where)/select_n | solution.py:19
  16.3 0.7 reshape.176
  17.0 1.0 %all-to-all-done = bf16[8,1,2]{2,1,0:T(2,128)(2,1)S(1)} async-done(((bf16[8,1,2]{2,1,0:T(2,128)(2,1)}), bf16[8,1,2]{2,1,0:T(2,128)(2,1)S(1)}, u32[]{:S(2)}, u32[]{:S(2)}) %all-to-all-start) | async-done | bytes 64 | tf_op jit(solution)/shard_map/all_to_all | solution.py:22
  18.0 0.1 copy.18
  18.2 0.2 reduce-window.8
  18.4 0.1 fusion.4
  18.5 3.4 %all-to-all-start.1 = ((bf16[8,2,3584]{2,1,0:T(2,128)(2,1)}), bf16[8,2,3584]{2,1,0:T(2,128)(2,1)S(1)}, u32[]{:S(2)}, u32[]{:S(2)}) async-start(bf16[8,2,3584]{2,1,0:T(2,128)(2,1)} %reshape.176), calls=%async_computation.1 | async-start | bytes 229376 | tf_op jit(solution)/shard_map/all_to_all | solution.py:21
  21.9 0.0 reduce-scatter.2.cloned.1.call-start
  21.9 11.2 %all-gather = bf16[4,8,2]{1,2,0:T(2,128)(2,1)S(1)} all-gather(bf16[1,8,2]{1,2,0:T(2,128)(2,1)S(1)} %fusion.4), channel_id=1, replica_groups=mesh['node'=8,'local'=4] {'local'}, dimensions={0}, use_global_device_ids=true | all-gather | bytes 160 | tf_op jit(solution)/shard_map/all_gather | solution.py:39
  33.1 0.1 reshape.172
  33.2 0.0 all-to-all-done.1
  33.2 0.1 reshape.177
  33.3 0.2 convolution_convert_fusion.1
  33.4 14.5 %all_gather.6 = bf16[32,7168]{1,0:T(8,128)(2,1)S(1)} all-gather(bf16[8,7168]{1,0:T(8,128)(2,1)S(1)} %convolution_convert_fusion.1), channel_id=1, replica_groups=mesh['node'=8,'local'=4] {'local'}, dimensions={0}, use_global_device_ids=true | all-gather | bytes 573440 | tf_op jit(solution)/shard_map/all_gather | solution.py:38
  47.9 5.4 %fusion.7 = f32[32,2,256]{2,0,1:T(8,128)S(1)} fusion(bf16[2,256,7168]{2,1,0:T(8,128)(2,1)} %param.7, bf16[32,7168]{1,0:T(8,128)(2,1)S(1)} %all_gather.6), kind=kOutput, calls=%fused_computation.11 | convolution fusion | flops 234881024 | bytes 7864320 | tf_op jit(solution)/shard_map/rd,efd->ref/dot_general | solution.py:41
  53.2 9.6 %fusion = bf16[32,7168]{1,0:T(8,128)(2,1)} fusion(bf16[2,256,7168]{2,1,0:T(8,128)(2,1)} %param.9, bf16[2,256,7168]{2,1,0:T(8,128)(2,1)} %param.8, bf16[32,7168]{1,0:T(8,128)(2,1)S(1)} %all_gather.6, f32[32,2,256]{2,0,1:T(8,128)S(1)} %fusion.7, f32[32,2]{0,1:T(2,128)S(1)} %reshape.172), kind=kOutput, calls=%fused_computation.1 | convolution fusion | flops 470106112 | bytes 15663360 | tf_op jit(solution)/shard_map/dot_general | solution.py:47
  62.9 0.0 reduce-scatter.2.cloned.1.call-update
  62.9 20.2 %reduce-scatter.2.cloned.1.call-done = bf16[8,7168]{1,0:T(8,128)(2,1)} async-done(((bf16[32,7168]{1,0:T(8,128)(2,1)}), bf16[8,7168]{1,0:T(8,128)(2,1)}) %reduce-scatter.2.cloned.1.call-update) | async-done | bytes 114704 | tf_op jit(solution)/shard_map/reduce_scatter | solution.py:48
  83.1 1.1 %fusion.1 = bf16[8,1,7168]{2,0,1:T(8,128)(2,1)S(1)} fusion(bf16[8,7168]{1,0:T(8,128)(2,1)} %reduce-scatter.2.cloned.1.call-done, s32[8]{0:T(128)S(1)} %bitcast_subtract_fusion, pred[8]{0:T(512)(128)(4,1)S(1)} %get-tuple-element.7), kind=kOutput, calls=%fused_computation.4 | convolution fusion | flops 974976 | bytes 229416 | tf_op jit(solution)/shard_map/dot_general | solution.py:51
  84.2 0.6 reduce.7
  84.9 0.1 reshape.178
  84.9 8.8 %all_to_all.15 = bf16[8,2,3584]{2,1,0:T(2,128)(2,1)S(1)} all-to-all(bf16[8,2,3584]{2,1,0:T(2,128)(2,1)S(1)} %reshape.178), channel_id=1, replica_groups=mesh['node'=8,'local'=4] {'node'}, dimensions={0} | all-to-all | bytes 229376 | tf_op jit(solution)/shard_map/all_to_all | solution.py:53
  93.7 0.1 reshape.179
  93.8 0.2 reduce_sum.44
  94.1 0.6 reduce_sum.45
  (7 shorter events, 0.1 us)
Async XLA Ops:
  8.2 9.8 %all-to-all-start = ((bf16[8,1,2]{2,1,0:T(2,128)(2,1)}), bf16[8,1,2]{2,1,0:T(2,128)(2,1)S(1)}, u32[]{:S(2)}, u32[]{:S(2)}) async-start(bf16[8,1,2]{2,1,0:T(2,128)(2,1)} %copy.17), calls=%async_computation | async-start | bytes 8192 | tf_op jit(solution)/shard_map/all_to_all | solution.py:22
  18.5 14.7 %all-to-all-start.1 = ((bf16[8,2,3584]{2,1,0:T(2,128)(2,1)}), bf16[8,2,3584]{2,1,0:T(2,128)(2,1)S(1)}, u32[]{:S(2)}, u32[]{:S(2)}) async-start(bf16[8,2,3584]{2,1,0:T(2,128)(2,1)} %reshape.176), calls=%async_computation.1 | async-start | bytes 229376 | tf_op jit(solution)/shard_map/all_to_all | solution.py:21
  21.9 61.2 %reduce-scatter.2.cloned.1.call-start = ((), (), s32[]{:S(2)}) async-start(), calls=%async_computation.4 | async-start | bytes 573440 | tf_op jit(solution)/shard_map/reduce_scatter | solution.py:48
Sparse Core Ops, SparseCore 0:
  63.0 20.0 reduce-scatter.1
where the time goes:
time: 102 us
  blocking collectives  34.4 us (34%)
  waiting for transfers between devices  21.3 us (21%)
  matrix products  16.4 us (16%)
  between operations  13.5 us (13%)
  starting transfers between devices  8.61 us (8%)
  other arithmetic  4.4 us (4%)
  local copies, waits for them, and re-layouts  2.97 us (3%)
    reduce_scatter x1, waiting for transfers between devices, on_device(): lax.psum_scatter(partial_value.astype(jnp.bfloat16), 'local', scatter_dim...  20.2 us
    all_gather x1, blocking collectives, on_device(): lax.all_gather(packed, 'local', axis=0, tiled=True)  14.5 us
    all_gather x1, blocking collectives, on_device(): lax.all_gather(packed_gates, 'local', axis=0, tiled=True)  11.2 us
    dot_general x1, matrix products, on_device(): jnp.dot(hidden, down_flat, preferred_element_type=jnp.float32)  9.61 us
    all_to_all x1, blocking collectives, on_device(): lax.all_to_all(unpacked, 'node', split_axis=0, concat_axis=0, tiled=True)  8.81 us
    dot_general x1, matrix products, on_device(): jnp.einsum('rd,efd->ref', all_rows, w_gate, preferred_element_type=jnp.fl...  5.37 us
    all_to_all x1, starting transfers between devices, on_device(): lax.all_to_all(gate_sums.astype(jnp.bfloat16), 'node', split_axis=0, conc...  5.2 us
    all_to_all x1, starting transfers between devices, on_device(): lax.all_to_all(outgoing, 'node', split_axis=0, concat_axis=0, tiled=True)  3.37 us
  transfers between devices with their start and end apart: 3, of which 2 were waited for; matrix products, arithmetic and copies ran while one was open for 4% of the time, Pallas kernels for 0%

commit v1 on v0

--- a/solution.py
+++ b/solution.py
@@ -1,6 +1,10 @@
+import functools
+
 import jax
 import jax.numpy as jnp
 from jax import lax
+from jax.experimental import pallas as pl
+from jax.experimental.pallas import tpu as pltpu
 from jax.sharding import PartitionSpec as P
 
 CAP = 8
@@ -54,9 +58,303 @@
     return jnp.sum(returned.astype(jnp.float32), axis=0).astype(jnp.bfloat16)
 
 
+LANES = 128
+BF16 = jnp.bfloat16
+F32 = jnp.float32
+
+
+def flip(value, mask):
+    bit = 1
+    out = value
+    while bit <= mask:
+        if mask & bit:
+            out = out + bit - 2 * bit * ((value // bit) % 2)
+        bit *= 2
+    return out
+
+
+def kernel(
+    nodes, locals_, tok_ref, ids_ref, gate_ints_ref, wg_hbm, wu_hbm, wd_hbm, out_ref,
+    wg, wu, wd, xbuf, xf, xs, acc, ps, pr, pf, qf, qs, r2, ss, r3, of,
+    w_sem, x_send, x_recv, p_send, p_recv, q_send, q_recv, s_send, s_recv,
+):
+    chips = nodes // 2
+    rows = nodes * locals_
+    half = rows // 2
+    width = tok_ref.shape[1]
+    pieces = width // LANES
+    pitch = xbuf.shape[1]
+    experts, ffl = wg.shape[0], wg.shape[1]
+    me_n = lax.axis_index("node")
+    me_l = lax.axis_index("local")
+
+    def peer(offset):
+        core, rest = offset // half, offset % half
+        chip, loc = rest // locals_, rest % locals_
+        return (flip(me_n, chip * 2 + core), flip(me_l, loc))
+
+    z_offsets = list(range(1, locals_))
+    c_offsets = [c * locals_ for c in range(1, chips)]
+    partner = half
+    barrier = pltpu.get_barrier_semaphore()
+    greeted = z_offsets + c_offsets + [partner]
+    for offset in greeted:
+        pl.semaphore_signal(
+            barrier, inc=1, device_id=peer(offset), device_id_type=pl.DeviceIdType.MESH
+        )
+
+    loads = []
+    for which, (source, dest) in enumerate(((wg_hbm, wg), (wu_hbm, wu), (wd_hbm, wd))):
+        for e in range(experts):
+            copy = pltpu.make_async_copy(source.at[e], dest.at[e], w_sem.at[which, e])
+            copy.start()
+            loads.append(copy)
+
+    xf[0:pitch, :] = jnp.zeros((pitch, LANES), F32)
+    for k in range(pieces):
+        xf[k : k + 1, :] = tok_ref[:, k * LANES : (k + 1) * LANES].astype(F32)
+    top = ids_ref.shape[1]
+    xf[pieces : pieces + 1, 0:top] = ids_ref[...].astype(F32)
+    xf[pieces + 1 : pieces + 2, 0:top] = gate_ints_ref[...].astype(F32)
+    xbuf[0] = xf[0:pitch, :].astype(BF16)
+
+    pl.semaphore_wait(barrier, len(greeted))
+
+    waits = []
+
+    def send(row, offset, slot):
+        copy = pltpu.make_async_remote_copy(
+            src_ref=xbuf.at[row],
+            dst_ref=xbuf.at[row ^ offset],
+            send_sem=x_send.at[slot, row],
+            recv_sem=x_recv.at[row ^ offset],
+            device_id=peer(offset),
+            device_id_type=pl.DeviceIdType.MESH,
+        )
+        copy.start()
+        waits.append(copy)
+
+    def arrive(row):
+        pltpu.make_async_remote_copy(
+            src_ref=xbuf.at[row],
+            dst_ref=xbuf.at[row],
+            send_sem=x_send.at[0, row],
+            recv_sem=x_recv.at[row],
+            device_id=peer(partner),
+            device_id_type=pl.DeviceIdType.MESH,
+        ).wait_recv()
+
+    def widen(row):
+        xf[row * pitch : (row + 1) * pitch, :] = xbuf[row].astype(F32)
+
+    for number, offset in enumerate(z_offsets):
+        send(0, offset, 1 + chips + number)
+    for number, offset in enumerate(c_offsets):
+        send(0, offset, 1 + number)
+    send(0, partner, 0)
+    for row in z_offsets:
+        arrive(row)
+        for number, offset in enumerate(c_offsets):
+            send(row, offset, 1 + number)
+        send(row, partner, 0)
+        widen(row)
+    for loc in range(locals_):
+        for offset in c_offsets:
+            row = offset + loc
+            arrive(row)
+            send(row, partner, 0)
+            widen(row)
+    for loc in range(locals_):
+        for offset in [0] + c_offsets:
+            arrive(half + offset + loc)
+            widen(half + offset + loc)
+
+    for k in range(pieces):
+        xs[:, k * LANES : (k + 1) * LANES] = xf[pl.ds(k, rows, stride=pitch), :].astype(BF16)
+    ids = xf[pl.ds(pieces, rows, stride=pitch), :]
+    gates = xf[pl.ds(pieces + 1, rows, stride=pitch), :]
+    scales = []
+    for e in range(experts):
+        named = (me_n * experts + e).astype(F32)
+        picked = jnp.where(ids == named, gates, 0.0)
+        scales.append(jnp.sum(picked, axis=1, keepdims=True) / 8.0)
+
+    for copy in loads[: 2 * experts]:
+        copy.wait()
+    chunk = 1024 if width % 1024 == 0 else width
+    acc[...] = jnp.zeros_like(acc)
+
+    def depth_step(step, carry):
+        at = pl.ds(pl.multiple_of(step * chunk, chunk), chunk)
+        x = xs[:, at]
+        for which, weights in enumerate((wg, wu)):
+            for e in range(experts):
+                acc[which, e] += lax.dot_general(
+                    weights[e, :, at], x, (((1,), (1,)), ((), ())), preferred_element_type=F32
+                )
+        return carry
+
+    lax.fori_loop(0, width // chunk, depth_step, 0)
+    hidden = []
+    for e in range(experts):
+        g = acc[0, e].T
+        u = acc[1, e].T
+        hidden.append((g / (1.0 + jnp.exp(-g)) * u * scales[e]).astype(BF16))
+
+    for copy in loads[2 * experts :]:
+        copy.wait()
+    sends = []
+    steps = width // chunk
+
+    def partner_copy(step):
+        at = pl.ds(step * chunk, chunk)
+        return pltpu.make_async_remote_copy(
+            src_ref=ps.at[:, at],
+            dst_ref=pr.at[:, at],
+            send_sem=p_send.at[step],
+            recv_sem=p_recv.at[step],
+            device_id=peer(partner),
+            device_id_type=pl.DeviceIdType.MESH,
+        )
+
+    for step in range(steps):
+        at = slice(step * chunk, (step + 1) * chunk)
+        part = jnp.dot(hidden[0], wd[0, :, at], preferred_element_type=F32)
+        for e in range(1, experts):
+            part += jnp.dot(hidden[e], wd[e, :, at], preferred_element_type=F32)
+        ps[:, at] = part[half:].astype(BF16)
+        pf[:, at] = part[:half]
+        sends.append(partner_copy(step))
+        if step:
+            sends[step - 1].start()
+    sends[-1].start()
+    for step in range(steps):
+        sends[step].wait_recv()
+        at = slice(step * chunk, (step + 1) * chunk)
+        both = pf[:, at] + pr[:, at].astype(F32)
+        for k in range(chunk // LANES):
+            qf[pl.ds(step * (chunk // LANES) + k, half, stride=pitch), :] = both[
+                :, k * LANES : (k + 1) * LANES
+            ]
+
+    out_copies = []
+    for number, offset in list(enumerate(c_offsets))[::-1]:
+        for loc in range(locals_):
+            row = offset + loc
+            qs[number, loc] = qf[row * pitch : row * pitch + pieces, :].astype(BF16)
+        copy = pltpu.make_async_remote_copy(
+            src_ref=qs.at[number],
+            dst_ref=r2.at[number],
+            send_sem=q_send.at[number],
+            recv_sem=q_recv.at[number],
+            device_id=peer(offset),
+            device_id_type=pl.DeviceIdType.MESH,
+        )
+        copy.start()
+        out_copies.append(copy)
+    for copy in out_copies:
+        copy.wait_recv()
+    z_copies = []
+    for loc in list(range(locals_))[::-1]:
+        total = qf[loc * pitch : loc * pitch + pieces, :]
+        for number in range(chips - 1):
+            total += r2[number, loc].astype(F32)
+        if loc == 0:
+            of[...] = total
+        else:
+            ss[loc - 1] = total.astype(BF16)
+            copy = pltpu.make_async_remote_copy(
+                src_ref=ss.at[loc - 1],
+                dst_ref=r3.at[loc - 1],
+                send_sem=s_send.at[loc - 1],
+                recv_sem=s_recv.at[loc - 1],
+                device_id=peer(loc),
+                device_id_type=pl.DeviceIdType.MESH,
+            )
+            copy.start()
+            z_copies.append(copy)
+    total = of[...]
+    for copy in z_copies:
+        copy.wait_recv()
+    for loc in range(1, locals_):
+        total += r3[loc - 1].astype(F32)
+    out_ref[...] = total.astype(BF16)
+    for copy in waits + sends + out_copies + z_copies:
+        copy.wait_send()
+
+
+def fused(nodes, locals_, tokens, w_gate, w_up, w_down, expert_ids, gate_ints):
+    width = tokens.shape[1]
+    experts, ffl = w_gate.shape[0], w_gate.shape[1]
+    chips = nodes // 2
+    rows = nodes * locals_
+    half = rows // 2
+    pieces = width // LANES
+    pitch = -(-(pieces + 2) // 16) * 16
+    steps = width // 1024 if width % 1024 == 0 else 1
+    vmem = pl.BlockSpec(memory_space=pltpu.VMEM)
+    hbm = pl.BlockSpec(memory_space=pl.ANY)
+    dma = pltpu.SemaphoreType.DMA
+    out = pl.pallas_call(
+        functools.partial(kernel, nodes, locals_),
+        out_shape=jax.ShapeDtypeStruct((pieces, LANES), BF16),
+        in_specs=[vmem] * 3 + [hbm] * 3,
+        out_specs=vmem,
+        scratch_shapes=[
+            pltpu.VMEM((experts, ffl, width), BF16),
+            pltpu.VMEM((experts, ffl, width), BF16),
+            pltpu.VMEM((experts, ffl, width), BF16),
+            pltpu.VMEM((rows, pitch, LANES), BF16),
+            pltpu.VMEM((rows * pitch, LANES), F32),
+            pltpu.VMEM((rows, width), BF16),
+            pltpu.VMEM((2, experts, ffl, rows), F32),
+            pltpu.VMEM((half, width), BF16),
+            pltpu.VMEM((half, width), BF16),
+            pltpu.VMEM((half, width), F32),
+            pltpu.VMEM((half * pitch, LANES), F32),
+            pltpu.VMEM((chips - 1, locals_, pieces, LANES), BF16),
+            pltpu.VMEM((chips - 1, locals_, pieces, LANES), BF16),
+            pltpu.VMEM((locals_ - 1, pieces, LANES), BF16),
+            pltpu.VMEM((locals_ - 1, pieces, LANES), BF16),
+            pltpu.VMEM((pieces, LANES), F32),
+            dma((3, experts)),
+            dma((chips + locals_, rows)),
+            dma((rows,)),
+            dma((steps,)),
+            dma((steps,)),
+            dma((chips - 1,)),
+            dma((chips - 1,)),
+            dma((locals_ - 1,)),
+            dma((locals_ - 1,)),
+        ],
+        compiler_params=pltpu.CompilerParams(
+            collective_id=0, has_side_effects=True, vmem_limit_bytes=56 * 1024 * 1024
+        ),
+    )(tokens, expert_ids, gate_ints, w_gate, w_up, w_down)
+    return out.reshape(1, width)
+
+
+def route(nodes, locals_, tokens, w_gate, w_up, w_down, expert_ids, gate_ints):
+    width = tokens.shape[1]
+    power = (nodes & (nodes - 1)) == 0 and (locals_ & (locals_ - 1)) == 0
+    small = (
+        nodes * tokens.shape[0] <= CAP
+        and tokens.shape[0] == 1
+        and nodes >= 4
+        and locals_ >= 2
+        and nodes * w_gate.shape[0] <= 256
+        and (nodes * locals_) % 32 == 0
+        and width % LANES == 0
+        and 3 * w_gate.size * 2 <= 32 * 1024 * 1024
+    )
+    if power and small:
+        return fused(nodes, locals_, tokens, w_gate, w_up, w_down, expert_ids, gate_ints)
+    return on_device(tokens, w_gate, w_up, w_down, expert_ids, gate_ints)
+
+
 def solution(mesh):
     return jax.shard_map(
-        on_device,
+        functools.partial(route, mesh.shape["node"], mesh.shape["local"]),
         mesh=mesh,
         in_specs=(
             P(("node", "local"), None),

time: 102 us -> 35.9 us (0.35)
  blocking collectives: 34.4 us -> 0 us
  Pallas kernels: 0 us -> 34.3 us
  waiting for transfers between devices: 21.3 us -> 0 us
  matrix products: 16.4 us -> 0 us
  between operations: 13.5 us -> 0.01 us
  starting transfers between devices: 8.61 us -> 0 us
  other arithmetic: 4.4 us -> 0 us
  local copies, waits for them, and re-layouts: 2.97 us -> 1.34 us
    pallas_call x0 -> x1, Pallas kernels: none -> 34.3 us  [fused(): pl.pallas_call(functools.partial(kernel, nodes, locals_), out_shape=jax.S...]
    all_gather x2 -> x0, blocking collectives: 25.6 us -> none  [the longest x1 14.5 us: on_device(): lax.all_gather(packed, 'local', axis=0, tiled=True)]
    reduce_scatter x1 -> x0, waiting for transfers between devices: 20.2 us -> none  [on_device(): lax.psum_scatter(partial_value.astype(jnp.bfloat16), 'local', scatter_dim...]
    dot_general x5 -> x0, matrix products: 16.4 us -> none  [the longest x1 9.61 us: on_device(): jnp.dot(hidden, down_flat, preferred_element_type=jnp.float32)]
    all_to_all x1 -> x0, blocking collectives: 8.81 us -> none  [on_device(): lax.all_to_all(unpacked, 'node', split_axis=0, concat_axis=0, tiled=True)]
    all_to_all x2 -> x0, starting transfers between devices: 8.57 us -> none  [the longest x1 5.2 us: on_device(): lax.all_to_all(gate_sums.astype(jnp.bfloat16), 'node', split_axis=0, conc...]
    select_n x2 -> x0, other arithmetic: 1.48 us -> none  [on_device(): jnp.where(is_hit[:, :, None], tokens[None, :, :], jnp.zeros_like(tokens)[...]
    reduce_sum x3 -> x0, other arithmetic: 1.25 us -> none  [the longest x1 0.98 us: on_device(): jnp.sum(jnp.where(matched, gate_ints[None, :, :, None], 0), axis=2)]
  transfers between devices with their start and end apart: 3 -> 0, of which waited for: 2 -> 0; matrix products, arithmetic and copies ran while one was open for 4% -> 0% of each run, Pallas kernels for 0% -> 0%
where the time goes in v1:
time: 35.9 us; the launch traced here: 35.6 us
  Pallas kernels  34.3 us (96%)
  local copies, waits for them, and re-layouts  1.34 us (4%)
    pallas_call x1, Pallas kernels, fused(): pl.pallas_call(functools.partial(kernel, nodes, locals_), out_shape=jax.S...  34.3 us
    unnamed x1, local copies, waits for them, and re-layouts  1.34 us

profile of v1, /device:TPU:0, one launch (start us, length us, event | category | flops | bytes accessed | tf_op | source)
XLA Modules:
  0.0 35.6 jit_solution(13670597893110174095)
XLA Ops:
  0.0 34.3 %shard_map.64 = bf16[56,128]{1,0:T(8,128)(2,1)} custom-call(bf16[1,7168]{1,0:T(2,128)(2,1)} %tok_ref.1, s32[1,8]{1,0:T(1,128)} %ids_ref.1, s32[1,8]{1,0:T(1,128)} %gate_ints_ref.1, bf16[2,256,7168]{2,1,0:T(8,128)(2,1)} %wg_hbm.1, bf16[2,256,7168]{2,1,0:T(8,128)(2,1)} %wu_hbm.1, bf16[2,256,7168]{2,1,0:T(8,128)(2,1)} %wd_hbm.1), custom_call_target="tpu_custom_call" | custom-call | tf_op jit(solution)/shard_map/pallas_call | solution.py:298
  34.3 1.3 %copy.9 = bf16[1,1,56,128]{3,1,2,0:T(2,128)(2,1)} copy(bf16[1,1,56,128]{3,2,1,0:T(8,128)(2,1)} %bitcast.5) | data formatting | bytes 28672

commit v2 on v1

--- a/solution.py
+++ b/solution.py
@@ -74,17 +74,19 @@
 
 
 def kernel(
-    nodes, locals_, tok_ref, ids_ref, gate_ints_ref, wg_hbm, wu_hbm, wd_hbm, out_ref,
-    wg, wu, wd, xbuf, xf, xs, acc, ps, pr, pf, qf, qs, r2, ss, r3, of,
+    nodes, locals_, tok_hbm, ids_hbm, gate_ints_hbm, wg_hbm, wu_hbm, wd_hbm, out_ref,
+    tok_ref, ids_ref, gate_ints_ref, in_sem, wgu, wd, xbuf, xf, xs, acc, ps, pr, pf, qf, qs, r2, ss, r3, of,
     w_sem, x_send, x_recv, p_send, p_recv, q_send, q_recv, s_send, s_recv,
 ):
     chips = nodes // 2
     rows = nodes * locals_
     half = rows // 2
-    width = tok_ref.shape[1]
+    width = tok_hbm.shape[1]
+    chunk = 1024 if width % 1024 == 0 else width
+    deep = 1792 if width % 1792 == 0 else chunk
     pieces = width // LANES
     pitch = xbuf.shape[1]
-    experts, ffl = wg.shape[0], wg.shape[1]
+    experts, ffl = wg_hbm.shape[0], wg_hbm.shape[1]
     me_n = lax.axis_index("node")
     me_l = lax.axis_index("local")
 
@@ -103,14 +105,16 @@
             barrier, inc=1, device_id=peer(offset), device_id_type=pl.DeviceIdType.MESH
         )
 
-    loads = []
-    for which, (source, dest) in enumerate(((wg_hbm, wg), (wu_hbm, wu), (wd_hbm, wd))):
-        for e in range(experts):
-            copy = pltpu.make_async_copy(source.at[e], dest.at[e], w_sem.at[which, e])
-            copy.start()
-            loads.append(copy)
-
+    small = []
+    for which, (source, dest) in enumerate(
+        ((tok_hbm, tok_ref), (ids_hbm, ids_ref), (gate_ints_hbm, gate_ints_ref))
+    ):
+        copy = pltpu.make_async_copy(source, dest, in_sem.at[which])
+        copy.start()
+        small.append(copy)
     xf[0:pitch, :] = jnp.zeros((pitch, LANES), F32)
+    for copy in small:
+        copy.wait()
     for k in range(pieces):
         xf[k : k + 1, :] = tok_ref[:, k * LANES : (k + 1) * LANES].astype(F32)
     top = ids_ref.shape[1]
@@ -122,22 +126,26 @@
 
     waits = []
 
-    def send(row, offset, slot):
-        copy = pltpu.make_async_remote_copy(
-            src_ref=xbuf.at[row],
-            dst_ref=xbuf.at[row ^ offset],
+    def block_copy(row, count, offset, slot):
+        landing = row ^ offset if count == 1 else (row // locals_ * locals_ ^ offset) + row % locals_
+        return pltpu.make_async_remote_copy(
+            src_ref=xbuf.at[pl.ds(row, count)],
+            dst_ref=xbuf.at[pl.ds(landing, count)],
             send_sem=x_send.at[slot, row],
-            recv_sem=x_recv.at[row ^ offset],
+            recv_sem=x_recv.at[landing],
             device_id=peer(offset),
             device_id_type=pl.DeviceIdType.MESH,
         )
+
+    def send(row, count, offset, slot):
+        copy = block_copy(row, count, offset, slot)
         copy.start()
         waits.append(copy)
 
-    def arrive(row):
+    def arrive(row, count):
         pltpu.make_async_remote_copy(
-            src_ref=xbuf.at[row],
-            dst_ref=xbuf.at[row],
+            src_ref=xbuf.at[pl.ds(row, count)],
+            dst_ref=xbuf.at[pl.ds(row, count)],
             send_sem=x_send.at[0, row],
             recv_sem=x_recv.at[row],
             device_id=peer(partner),
@@ -147,27 +155,36 @@
     def widen(row):
         xf[row * pitch : (row + 1) * pitch, :] = xbuf[row].astype(F32)
 
-    for number, offset in enumerate(z_offsets):
-        send(0, offset, 1 + chips + number)
+    for number, offset in list(enumerate(z_offsets))[::-1]:
+        send(0, 1, offset, 1 + chips + number)
     for number, offset in enumerate(c_offsets):
-        send(0, offset, 1 + number)
-    send(0, partner, 0)
+        send(0, 1, offset, 1 + number)
+    send(0, 1, partner, 0)
+    loads = []
+    places = ((wg_hbm, wgu, 0), (wu_hbm, wgu, experts), (wd_hbm, wd, 0))
+    for which, (source, dest, first) in enumerate(places):
+        for e in range(experts):
+            copy = pltpu.make_async_copy(
+                source.at[e], dest.at[pl.ds((first + e) * ffl, ffl)], w_sem.at[which, e]
+            )
+            copy.start()
+            loads.append(copy)
+
     for row in z_offsets:
-        arrive(row)
+        arrive(row, 1)
         for number, offset in enumerate(c_offsets):
-            send(row, offset, 1 + number)
-        send(row, partner, 0)
+            send(row, 1, offset, 1 + number)
+        send(row, 1, partner, 0)
         widen(row)
     for loc in range(locals_):
         for offset in c_offsets:
             row = offset + loc
-            arrive(row)
-            send(row, partner, 0)
+            arrive(row, 1)
+            send(row, 1, partner, 0)
             widen(row)
-    for loc in range(locals_):
-        for offset in [0] + c_offsets:
-            arrive(half + offset + loc)
-            widen(half + offset + loc)
+    for row in range(half, rows):
+        arrive(row, 1)
+        widen(row)
 
     for k in range(pieces):
         xs[:, k * LANES : (k + 1) * LANES] = xf[pl.ds(k, rows, stride=pitch), :].astype(BF16)
@@ -181,25 +198,22 @@
 
     for copy in loads[: 2 * experts]:
         copy.wait()
-    chunk = 1024 if width % 1024 == 0 else width
     acc[...] = jnp.zeros_like(acc)
 
     def depth_step(step, carry):
-        at = pl.ds(pl.multiple_of(step * chunk, chunk), chunk)
-        x = xs[:, at]
-        for which, weights in enumerate((wg, wu)):
-            for e in range(experts):
-                acc[which, e] += lax.dot_general(
-                    weights[e, :, at], x, (((1,), (1,)), ((), ())), preferred_element_type=F32
-                )
+        at = pl.ds(pl.multiple_of(step * deep, deep), deep)
+        acc[...] += lax.dot_general(
+            wgu[:, at], xs[:, at], (((1,), (1,)), ((), ())), preferred_element_type=F32
+        )
         return carry
 
-    lax.fori_loop(0, width // chunk, depth_step, 0)
+    lax.fori_loop(0, width // deep, depth_step, 0)
     hidden = []
     for e in range(experts):
-        g = acc[0, e].T
-        u = acc[1, e].T
+        g = acc[e * ffl : (e + 1) * ffl, :].T
+        u = acc[(experts + e) * ffl : (experts + e + 1) * ffl, :].T
         hidden.append((g / (1.0 + jnp.exp(-g)) * u * scales[e]).astype(BF16))
+    hidden = jnp.concatenate(hidden, axis=1)
 
     for copy in loads[2 * experts :]:
         copy.wait()
@@ -217,68 +231,86 @@
             device_id_type=pl.DeviceIdType.MESH,
         )
 
-    for step in range(steps):
-        at = slice(step * chunk, (step + 1) * chunk)
-        part = jnp.dot(hidden[0], wd[0, :, at], preferred_element_type=F32)
-        for e in range(1, experts):
-            part += jnp.dot(hidden[e], wd[e, :, at], preferred_element_type=F32)
-        ps[:, at] = part[half:].astype(BF16)
-        pf[:, at] = part[:half]
-        sends.append(partner_copy(step))
-        if step:
-            sends[step - 1].start()
-    sends[-1].start()
-    for step in range(steps):
+    per = chunk // LANES
+    first_group = (steps + 1) // 2
+    groups = [(0, first_group), (first_group, steps)]
+    groups = [(low, high) for low, high in groups if high > low]
+    out_copies = []
+    z_copies = []
+
+    def combine(step):
         sends[step].wait_recv()
         at = slice(step * chunk, (step + 1) * chunk)
         both = pf[:, at] + pr[:, at].astype(F32)
-        for k in range(chunk // LANES):
-            qf[pl.ds(step * (chunk // LANES) + k, half, stride=pitch), :] = both[
+        for k in range(per):
+            qf[pl.ds(step * per + k, half, stride=pitch), :] = both[
                 :, k * LANES : (k + 1) * LANES
             ]
 
-    out_copies = []
-    for number, offset in list(enumerate(c_offsets))[::-1]:
-        for loc in range(locals_):
-            row = offset + loc
-            qs[number, loc] = qf[row * pitch : row * pitch + pieces, :].astype(BF16)
-        copy = pltpu.make_async_remote_copy(
-            src_ref=qs.at[number],
-            dst_ref=r2.at[number],
-            send_sem=q_send.at[number],
-            recv_sem=q_recv.at[number],
-            device_id=peer(offset),
-            device_id_type=pl.DeviceIdType.MESH,
-        )
-        copy.start()
-        out_copies.append(copy)
-    for copy in out_copies:
-        copy.wait_recv()
-    z_copies = []
-    for loc in list(range(locals_))[::-1]:
-        total = qf[loc * pitch : loc * pitch + pieces, :]
-        for number in range(chips - 1):
-            total += r2[number, loc].astype(F32)
-        if loc == 0:
-            of[...] = total
-        else:
-            ss[loc - 1] = total.astype(BF16)
+    def send_chips(group):
+        low, high = groups[group][0] * per, groups[group][1] * per
+        for number, offset in list(enumerate(c_offsets))[::-1]:
+            for loc in range(locals_):
+                at = (offset + loc) * pitch
+                qs[group, number, loc, 0 : high - low] = qf[at + low : at + high, :].astype(BF16)
             copy = pltpu.make_async_remote_copy(
-                src_ref=ss.at[loc - 1],
-                dst_ref=r3.at[loc - 1],
-                send_sem=s_send.at[loc - 1],
-                recv_sem=s_recv.at[loc - 1],
-                device_id=peer(loc),
+                src_ref=qs.at[group, number, :, pl.ds(0, high - low)],
+                dst_ref=r2.at[group, number, :, pl.ds(0, high - low)],
+                send_sem=q_send.at[group, number],
+                recv_sem=q_recv.at[group, number],
+                device_id=peer(offset),
                 device_id_type=pl.DeviceIdType.MESH,
             )
             copy.start()
-            z_copies.append(copy)
-    total = of[...]
-    for copy in z_copies:
-        copy.wait_recv()
-    for loc in range(1, locals_):
-        total += r3[loc - 1].astype(F32)
-    out_ref[...] = total.astype(BF16)
+            out_copies.append(copy)
+
+    lag = 7
+    for step in range(steps + lag):
+        if step < steps:
+            at = slice(step * chunk, (step + 1) * chunk)
+            part = jnp.dot(hidden, wd[:, at], preferred_element_type=F32)
+            ps[:, at] = part[half:].astype(BF16)
+            pf[:, at] = part[:half]
+            sends.append(partner_copy(step))
+        if 1 <= step <= steps:
+            sends[step - 1].start()
+        if step >= lag:
+            combine(step - lag)
+            for group, (low, high) in enumerate(groups):
+                if step - lag == high - 1:
+                    send_chips(group)
+
+    for group, (first, last) in enumerate(groups):
+        low, high = first * per, last * per
+        for copy in out_copies[group * (chips - 1) : (group + 1) * (chips - 1)]:
+            copy.wait_recv()
+        for loc in list(range(locals_))[::-1]:
+            total = qf[loc * pitch + low : loc * pitch + high, :]
+            for number in range(chips - 1):
+                total += r2[group, number, loc, 0 : high - low].astype(F32)
+            if loc == 0:
+                of[low:high, :] = total
+            else:
+                ss[group, loc - 1, 0 : high - low] = total.astype(BF16)
+                copy = pltpu.make_async_remote_copy(
+                    src_ref=ss.at[group, loc - 1, pl.ds(0, high - low)],
+                    dst_ref=r3.at[group, loc - 1, pl.ds(0, high - low)],
+                    send_sem=s_send.at[group, loc - 1],
+                    recv_sem=s_recv.at[group, loc - 1],
+                    device_id=peer(loc),
+                    device_id_type=pl.DeviceIdType.MESH,
+                )
+                copy.start()
+                z_copies.append(copy)
+    for group, (first, last) in enumerate(groups):
+        low, high = first * per, last * per
+        total = of[low:high, :]
+        for copy in z_copies[group * (locals_ - 1) : (group + 1) * (locals_ - 1)]:
+            copy.wait_recv()
+        for loc in range(1, locals_):
+            total += r3[group, loc - 1, 0 : high - low].astype(F32)
+        for k in range(high - low):
+            out_ref[:, (low + k) * LANES : (low + k + 1) * LANES] = total[k : k + 1, :].astype(BF16)
     for copy in waits + sends + out_copies + z_copies:
         copy.wait_send()
 
@@ -292,46 +324,49 @@
     pieces = width // LANES
     pitch = -(-(pieces + 2) // 16) * 16
     steps = width // 1024 if width % 1024 == 0 else 1
+    most = (steps + 1) // 2 * (width // steps // LANES)
     vmem = pl.BlockSpec(memory_space=pltpu.VMEM)
     hbm = pl.BlockSpec(memory_space=pl.ANY)
     dma = pltpu.SemaphoreType.DMA
-    out = pl.pallas_call(
+    return pl.pallas_call(
         functools.partial(kernel, nodes, locals_),
-        out_shape=jax.ShapeDtypeStruct((pieces, LANES), BF16),
-        in_specs=[vmem] * 3 + [hbm] * 3,
+        out_shape=jax.ShapeDtypeStruct((1, width), BF16),
+        in_specs=[hbm] * 6,
         out_specs=vmem,
         scratch_shapes=[
-            pltpu.VMEM((experts, ffl, width), BF16),
-            pltpu.VMEM((experts, ffl, width), BF16),
-            pltpu.VMEM((experts, ffl, width), BF16),
+            pltpu.VMEM(tokens.shape, BF16),
+            pltpu.VMEM(expert_ids.shape, jnp.int32),
+            pltpu.VMEM(gate_ints.shape, jnp.int32),
+            dma((3,)),
+            pltpu.VMEM((2 * experts * ffl, width), BF16),
+            pltpu.VMEM((experts * ffl, width), BF16),
             pltpu.VMEM((rows, pitch, LANES), BF16),
             pltpu.VMEM((rows * pitch, LANES), F32),
             pltpu.VMEM((rows, width), BF16),
-            pltpu.VMEM((2, experts, ffl, rows), F32),
+            pltpu.VMEM((2 * experts * ffl, rows), F32),
             pltpu.VMEM((half, width), BF16),
             pltpu.VMEM((half, width), BF16),
             pltpu.VMEM((half, width), F32),
             pltpu.VMEM((half * pitch, LANES), F32),
-            pltpu.VMEM((chips - 1, locals_, pieces, LANES), BF16),
-            pltpu.VMEM((chips - 1, locals_, pieces, LANES), BF16),
-            pltpu.VMEM((locals_ - 1, pieces, LANES), BF16),
-            pltpu.VMEM((locals_ - 1, pieces, LANES), BF16),
+            pltpu.VMEM((2, chips - 1, locals_, most, LANES), BF16),
+            pltpu.VMEM((2, chips - 1, locals_, most, LANES), BF16),
+            pltpu.VMEM((2, locals_ - 1, most, LANES), BF16),
+            pltpu.VMEM((2, locals_ - 1, most, LANES), BF16),
             pltpu.VMEM((pieces, LANES), F32),
             dma((3, experts)),
             dma((chips + locals_, rows)),
             dma((rows,)),
             dma((steps,)),
             dma((steps,)),
-            dma((chips - 1,)),
-            dma((chips - 1,)),
-            dma((locals_ - 1,)),
-            dma((locals_ - 1,)),
+            dma((2, chips - 1)),
+            dma((2, chips - 1)),
+            dma((2, locals_ - 1)),
+            dma((2, locals_ - 1)),
         ],
         compiler_params=pltpu.CompilerParams(
             collective_id=0, has_side_effects=True, vmem_limit_bytes=56 * 1024 * 1024
         ),
     )(tokens, expert_ids, gate_ints, w_gate, w_up, w_down)
-    return out.reshape(1, width)
 
 
 def route(nodes, locals_, tokens, w_gate, w_up, w_down, expert_ids, gate_ints):

time: 35.9 us -> 34.3 us (0.955)
  Pallas kernels: 34.3 us -> 32.7 us
    pallas_call x1, Pallas kernels: 34.3 us -> 32.7 us  [fused(): pl.pallas_call(functools.partial(kernel, nodes, locals_), out_shape=jax.S...]
where the time goes in v2:
time: 34.3 us; the launch traced here: 34 us
  Pallas kernels  32.7 us (95%)
  local copies, waits for them, and re-layouts  1.39 us (4%)
    pallas_call x1, Pallas kernels, fused(): pl.pallas_call(functools.partial(kernel, nodes, locals_), out_shape=jax.S...  32.7 us
    unnamed x1, local copies, waits for them, and re-layouts  1.39 us

profile of v2, /device:TPU:0, one launch (start us, length us, event | category | flops | bytes accessed | tf_op | source)
XLA Modules:
  0.0 34.0 jit_solution(5034992162627508130)
XLA Ops:
  0.0 32.7 %shard_map.64 = bf16[1,7168]{1,0:T(2,128)(2,1)} custom-call(bf16[1,7168]{1,0:T(2,128)(2,1)} %tok_hbm.1, s32[1,8]{1,0:T(1,128)} %ids_hbm.1, s32[1,8]{1,0:T(1,128)} %gate_ints_hbm.1, bf16[2,256,7168]{2,1,0:T(8,128)(2,1)} %wg_hbm.1, bf16[2,256,7168]{2,1,0:T(8,128)(2,1)} %wu_hbm.1, bf16[2,256,7168]{2,1,0:T(8,128)(2,1)} %wd_hbm.1), custom_call_target="tpu_custom_call" | custom-call | tf_op jit(solution)/shard_map/pallas_call | solution.py:331
  32.7 1.4 %copy.8 = bf16[1,7168]{1,0:T(2,128)(2,1)} copy(bf16[1,7168]{1,0:T(2,128)(2,1)} %shard_map.64) | data formatting | bytes 28672
